TPU v7x, 8 devices: a whole 2x2x1 slice. The times are simulated.
8 devices in a mesh: mat: 2 (over z, y), dp: 4 (over x, core).
Axes of the slice: x: 2, y: 2, z: 1, core: 2. Of those that a mesh axis runs over, the one named last changes fastest.
Arguments:
- a_mat: bfloat16 [4096, 65536], P('mat', 'dp'), parts along dimension 0
Outputs:
- output: float32 [8, 3, 512, 512], P(('mat', 'dp')), parts along dimension 0
There are 2 independent parts. A program takes and returns all parts, laid end to end along the dimension named above; each array names one.
All inputs are finite; a program needn't handle non-finite values.
Results may differ from a plain program's by a relative error of at most 0.001.
Values are sent between devices in bfloat16 or wider.
A program may use at most 1 GiB of HBM per device.

v0:
```python
import jax
import jax.numpy as jnp
from jax import lax
from jax.sharding import PartitionSpec as P


def packed_partial(blocks):
    groups = blocks.shape[0]
    blk_rows = blocks.shape[1]
    half = groups // 2
    slots = half + 1
    doubled = jnp.concatenate([blocks, blocks], axis=0)
    dev_ids = lax.broadcasted_iota(jnp.int32, (groups, 1, 1), 0)

    def slot_step(slot, packed):
        partner = lax.dynamic_slice_in_dim(doubled, groups - slot, groups, axis=0)
        block_prod = jnp.einsum('gik,gjk->gij', blocks, partner, preferred_element_type=jnp.float32)
        flipped = jnp.where(dev_ids < slot, jnp.swapaxes(block_prod, 1, 2), block_prod)
        keep_mask = jnp.logical_or(slot < half, dev_ids < half)
        return lax.dynamic_update_index_in_dim(packed, jnp.where(keep_mask, flipped, 0.0), slot, axis=1)

    packed = jnp.zeros((groups, slots, blk_rows, blk_rows), jnp.float32)
    return lax.fori_loop(0, slots, slot_step, packed)


def solution(mesh):
    groups = mesh.shape['dp']

    def local_gram(a_local):
        n_rows, local_cols = a_local.shape
        blocks = a_local.reshape(groups, n_rows // groups, local_cols)
        return lax.psum_scatter(packed_partial(blocks), 'dp', scatter_dimension=0, tiled=True)

    return jax.shard_map(local_gram, mesh=mesh, in_specs=(P('mat', 'dp'),), out_specs=P(('mat', 'dp')), check_vma=False)
```

profile of v0, /device:TPU:1, one launch (start us, length us, event | category | flops | bytes accessed | tf_op | source)
XLA Modules:
  0.0 374.7 jit_solution(15408446533825223464)
XLA Ops:
  6.5 0.0 reduce-scatter.4.cloned.1.call-start
  6.5 87.4 %pad_maximum_fusion = bf16[8,512,16384]{2,1,0:T(8,128)(2,1)} fusion(bf16[4,512,16384]{2,1,0:T(8,128)(2,1)} %bitcast), kind=kLoop, calls=%fused_computation.9 | loop fusion | flops 67108864 | bytes 201326592 | tf_op jit(solution)/shard_map/concatenate | solution.py:12
  94.0 181.6 %while.17 = (s32[]{:T(128)}, f32[4,3,512,512]{3,2,1,0:T(8,128)}, bf16[8,512,16384]{2,1,0:T(8,128)(2,1)}, bf16[4,512,16384]{2,1,0:T(8,128)(2,1)}, s32[]{:T(128)},...) while((s32[]{:T(128)}, f32[4,3,512,512]{3,2,1,0:T(8,128)}, ...), condition=%wide.region_1.2_spmd.clone.clone, body=%wide.region_0.1_spmd.clone.clone.sunk | while | flops 34361835520 | bytes 159384240 | solution.py:23
  94.0 48.7 %fusion.15 = f32[4,512,512]{2,1,0:T(8,128)} fusion(bf16[4,512,16384]{2,1,0:T(8,128)(2,1)} %get-tuple-element.225, bf16[8,512,16384]{2,1,0:T(8,128)(2,1)} %get-tuple-element.224, s32[]{:T(128)S(6)} %select_n.60), kind=kOutput, calls=%fused_computation.1.clone.2 | convolution fusion | flops 34359738368 | bytes 138412032 | tf_op jit(solution)/shard_map/while/body/eval_jaxpr/gik,gjk->gij/dot_general | solution.py:17
  142.7 5.2 %copy.9 = f32[4,512,512]{1,2,0:T(8,128)} copy(f32[4,512,512]{2,1,0:T(8,128)} %fusion.15) | data formatting | bytes 8388608 | tf_op jit(solution)/shard_map/while/body/eval_jaxpr/gik,gjk->gij/dot_general | solution.py:17
  147.9 6.6 %bitcast_dynamic-update-slice_fusion.2 = f32[4,3,512,512]{3,2,1,0:T(8,128)} fusion(f32[4,3,512,512]{3,2,1,0:T(8,128)} %get-tuple-element.214, s32[]{:T(128)} %get-tuple-element.213, f32[4,512,512]{2,1,0:T(8,128)} %fusion.15, f32[4,512,512]{1,2,0:T(8,128)} %copy.9, pred[4]{0:T(512)(128)(4,1)S(1)} %get-tuple-element.202, ...), kind=kLoop, calls=%fused_computation.3.clone.1 | loop fusion | flops 2097152 | bytes 12583432 | tf_op jit(solution)/shard_map/while/body/eval_jaxpr/jit(dynamic_update_index_in_dim)/dynamic_update_slice | solution.py:20
  154.5 48.7 %fusion.15 = f32[4,512,512]{2,1,0:T(8,128)} fusion(bf16[4,512,16384]{2,1,0:T(8,128)(2,1)} %get-tuple-element.225, bf16[8,512,16384]{2,1,0:T(8,128)(2,1)} %get-tuple-element.224, s32[]{:T(128)S(6)} %select_n.60), kind=kOutput, calls=%fused_computation.1.clone.2 | convolution fusion | flops 34359738368 | bytes 138412032 | tf_op jit(solution)/shard_map/while/body/eval_jaxpr/gik,gjk->gij/dot_general | solution.py:17
  203.2 5.2 %copy.9 = f32[4,512,512]{1,2,0:T(8,128)} copy(f32[4,512,512]{2,1,0:T(8,128)} %fusion.15) | data formatting | bytes 8388608 | tf_op jit(solution)/shard_map/while/body/eval_jaxpr/gik,gjk->gij/dot_general | solution.py:17
  208.4 6.6 %bitcast_dynamic-update-slice_fusion.2 = f32[4,3,512,512]{3,2,1,0:T(8,128)} fusion(f32[4,3,512,512]{3,2,1,0:T(8,128)} %get-tuple-element.214, s32[]{:T(128)} %get-tuple-element.213, f32[4,512,512]{2,1,0:T(8,128)} %fusion.15, f32[4,512,512]{1,2,0:T(8,128)} %copy.9, pred[4]{0:T(512)(128)(4,1)S(1)} %get-tuple-element.202, ...), kind=kLoop, calls=%fused_computation.3.clone.1 | loop fusion | flops 2097152 | bytes 12583432 | tf_op jit(solution)/shard_map/while/body/eval_jaxpr/jit(dynamic_update_index_in_dim)/dynamic_update_slice | solution.py:20
  215.1 48.7 %fusion.15 = f32[4,512,512]{2,1,0:T(8,128)} fusion(bf16[4,512,16384]{2,1,0:T(8,128)(2,1)} %get-tuple-element.225, bf16[8,512,16384]{2,1,0:T(8,128)(2,1)} %get-tuple-element.224, s32[]{:T(128)S(6)} %select_n.60), kind=kOutput, calls=%fused_computation.1.clone.2 | convolution fusion | flops 34359738368 | bytes 138412032 | tf_op jit(solution)/shard_map/while/body/eval_jaxpr/gik,gjk->gij/dot_general | solution.py:17
  263.7 5.2 %copy.9 = f32[4,512,512]{1,2,0:T(8,128)} copy(f32[4,512,512]{2,1,0:T(8,128)} %fusion.15) | data formatting | bytes 8388608 | tf_op jit(solution)/shard_map/while/body/eval_jaxpr/gik,gjk->gij/dot_general | solution.py:17
  269.0 6.5 %bitcast_dynamic-update-slice_fusion.2 = f32[4,3,512,512]{3,2,1,0:T(8,128)} fusion(f32[4,3,512,512]{3,2,1,0:T(8,128)} %get-tuple-element.214, s32[]{:T(128)} %get-tuple-element.213, f32[4,512,512]{2,1,0:T(8,128)} %fusion.15, f32[4,512,512]{1,2,0:T(8,128)} %copy.9, pred[4]{0:T(512)(128)(4,1)S(1)} %get-tuple-element.202, ...), kind=kLoop, calls=%fused_computation.3.clone.1 | loop fusion | flops 2097152 | bytes 12583432 | tf_op jit(solution)/shard_map/while/body/eval_jaxpr/jit(dynamic_update_index_in_dim)/dynamic_update_slice | solution.py:20
  275.6 0.0 reduce-scatter.4.cloned.1.call-update
  275.6 92.3 %reduce-scatter.4.cloned.1.call-done = f32[1,3,512,512]{3,2,1,0:T(8,128)} async-done(((f32[4,3,512,512]{3,2,1,0:T(8,128)}), f32[1,3,512,512]{3,2,1,0:T(8,128)}) %reduce-scatter.4.cloned.1.call-update) | async-done | bytes 3145744
  (4 shorter events, 0.0 us)
Async XLA Ops:
  6.5 361.3 %reduce-scatter.4.cloned.1.call-start = ((), (), s32[]{:S(2)}) async-start(), calls=%async_computation.1 | async-start | bytes 15728640
Sparse Core Ops, SparseCore 0:
  275.7 92.1 reduce-scatter.3
where the time goes:
time: 376 us; the launch traced here: 375 us
  matrix products  146 us (39%)
  other arithmetic  107 us (28%)
  waiting for transfers between devices  92.3 us (25%)
  local copies, waits for them, and re-layouts  15.7 us (4%)
  between operations  13.4 us (4%)
    dot_general x3, matrix products, slot_step(): jnp.einsum('gik,gjk->gij', blocks, partner, preferred_element_type=jnp.fl...  146 us
    unnamed x2, waiting for transfers between devices  92.3 us
    concatenate x1, other arithmetic, packed_partial(): doubled = jnp.concatenate([blocks, blocks], axis=0)  87.4 us
    dynamic_update_slice x3, other arithmetic, slot_step(): lax.dynamic_update_index_in_dim(packed, jnp.where(keep_mask, flipped, 0.0...  19.7 us
    dot_general x3, local copies, waits for them, and re-layouts, slot_step(): jnp.einsum('gik,gjk->gij', blocks, partner, preferred_element_type=jnp.fl...  15.7 us
  transfers between devices with their start and end apart: 1, of which 1 were waited for; matrix products, arithmetic and copies ran while one was open for 0% of the time, Pallas kernels for 0%

commit v1 on v0

v1 whole, which is shorter than its diff:
```python
import functools

import jax
import jax.numpy as jnp
from jax import lax
from jax.experimental import pallas as pl
from jax.experimental.pallas import tpu as pltpu
from jax.sharding import PartitionSpec as P

BLK = 512
TILE = 256
CHUNK = 2048
DIAG = 3 * TILE
FULL = 4 * TILE

STEPS = (
    dict(diag=True, lhs=(0, 0), rhs=(0, 0), remote=(1, 1), owner=(0, 0), slot=(0, 0)),
    dict(diag=False, lhs=(1, 1), rhs=(0, 0), remote=(1, 1), owner=(1, 1), slot=(1, 1)),
    dict(diag=True, lhs=(1, 1), rhs=(1, 1), remote=(1, 1), owner=(1, 1), slot=(0, 0)),
    dict(diag=False, lhs=(0, 2), rhs=(2, 0), remote=(1, 1), owner=(0, 0), slot=(1, 2)),
    dict(diag=False, lhs=(0, 2), rhs=(2, 0), remote=(0, 1), owner=(0, 0), slot=(2, 1)),
    dict(diag=False, lhs=(1, 2), rhs=(2, 1), remote=(0, 1), owner=(0, 1), slot=(1, 2)),
    dict(diag=True, lhs=(2, 2), rhs=(2, 2), remote=(0, 0), owner=(0, 1), slot=(0, 0)),
    dict(diag=False, lhs=(0, 2), rhs=(2, 0), remote=(0, 0), owner=(1, 1), slot=(1, 1)),
    dict(diag=True, lhs=(0, 0), rhs=(0, 0), remote=(0, 0), owner=(1, 0), slot=(0, 0)),
    dict(diag=False, lhs=(1, 0), rhs=(0, 1), remote=(0, 0), owner=(1, 0), slot=(2, 1)),
)
LOADS = (((2, 0), 0), ((3, 1), 1), ((1, 2), 2), ((0, 3), 2), ((1, 2), 0))
NEEDS = {0: 0, 1: 1, 3: 2, 4: 3, 7: 4}
N_REMOTE = 6


def kernel(a_ref, out_ref, a_buf, part, pair, recv, own, load_sem, d2d_send, d2d_recv, ici_send, ici_recv, out_sem):
    n_chunks = a_ref.shape[1] // CHUNK
    me = lax.axis_index("dp")
    chip = me // 2
    core = me % 2
    peer = chip * 2 + (1 - core)

    def pick(two):
        return two[0] if two[0] == two[1] else two[0] * (1 - chip) + two[1] * chip

    def load(which, c):
        block, slot = LOADS[which]
        return pltpu.make_async_copy(
            a_ref.at[pl.ds(pl.multiple_of(pick(block) * BLK, BLK), BLK), pl.ds(pl.multiple_of(c * CHUNK, CHUNK), CHUNK)],
            a_buf.at[slot * n_chunks + c],
            load_sem.at[which * n_chunks + c],
        )

    for which in range(3):
        for c in range(n_chunks):
            load(which, c).start()

    barrier = pltpu.get_barrier_semaphore()
    for hop in range(1, 4):
        pl.semaphore_signal(barrier, inc=1, device_id={"dp": (me + hop) % 4}, device_id_type=pl.DeviceIdType.MESH)

    def rows_of(s):
        return DIAG if STEPS[s]["diag"] else FULL

    def pair_copy(s):
        half = rows_of(s) // 2
        return pltpu.make_async_remote_copy(
            src_ref=part.at[s % 2, pl.ds(pl.multiple_of((1 - core) * half, 128), half)],
            dst_ref=pair.at[s, pl.ds(0, half)],
            send_sem=d2d_send.at[s],
            recv_sem=d2d_recv.at[s],
            device_id={"dp": peer},
            device_id_type=pl.DeviceIdType.MESH,
        )

    def own_copy(s):
        rows = rows_of(s)
        return pltpu.make_async_remote_copy(
            src_ref=part.at[s % 2, pl.ds(0, rows)],
            dst_ref=own.at[pick(STEPS[s]["slot"]), pl.ds(0, rows)],
            send_sem=d2d_send.at[s],
            recv_sem=d2d_recv.at[s],
            device_id={"dp": peer},
            device_id_type=pl.DeviceIdType.MESH,
        )

    def link_copy(s):
        half = rows_of(s) // 2
        slot = pick(STEPS[s]["slot"])
        return pltpu.make_async_remote_copy(
            src_ref=pair.at[s, pl.ds(0, half)],
            dst_ref=recv.at[slot, pl.ds(pl.multiple_of(core * half, 128), half)],
            send_sem=ici_send.at[s],
            recv_sem=ici_recv.at[slot * 2 + core],
            device_id={"dp": (1 - chip) * 2 + STEPS[s]["owner"][1]},
            device_id_type=pl.DeviceIdType.MESH,
        )

    def link_wait(slot, half_id, half):
        pltpu.make_async_remote_copy(
            src_ref=pair.at[0, pl.ds(0, half)],
            dst_ref=recv.at[slot, pl.ds(half_id * half, half)],
            send_sem=ici_send.at[0],
            recv_sem=ici_recv.at[slot * 2 + half_id],
            device_id={"dp": peer},
            device_id_type=pl.DeviceIdType.MESH,
        ).wait_recv()

    def by_mode(s, remote_fn, own_fn):
        remote = STEPS[s]["remote"]
        if remote == (1, 1):
            remote_fn()
        elif remote == (0, 0):
            own_fn()
        else:
            pl.when(chip == 1)(remote_fn)
            pl.when(chip == 0)(own_fn)

    def after_pop(s):
        is_owner = core == pick(STEPS[s]["owner"])

        def own_fn():
            pl.when(jnp.logical_not(is_owner))(lambda: own_copy(s).start())

        by_mode(s, lambda: pair_copy(s).start(), own_fn)

    def reduce_step(s):
        rows = rows_of(s)
        half = rows // 2
        is_owner = core == pick(STEPS[s]["owner"])

        def remote_fn():
            pair_copy(s).wait()

            @pl.loop(0, half // 128)
            def _(i):
                to = pl.ds(pl.multiple_of(i * 128, 128), 128)
                pair[s, to] += part[s % 2, pl.ds(pl.multiple_of(core * half + i * 128, 128), 128)]

        def own_fn():
            @pl.when(is_owner)
            def _():
                own_copy(s).wait_recv()
                slot = pick(STEPS[s]["slot"])

                @pl.loop(0, rows // 128)
                def _(i):
                    to = pl.ds(pl.multiple_of(i * 128, 128), 128)
                    own[slot, to] += part[s % 2, to]

            @pl.when(jnp.logical_not(is_owner))
            def _():
                own_copy(s).wait_send()

        by_mode(s, remote_fn, own_fn)

    def send_step(s):
        by_mode(s, lambda: link_copy(s).start(), lambda: None)

    def dot(lhs, rhs):
        return lax.dot_general(lhs, rhs, (((1,), (1,)), ((), ())), preferred_element_type=jnp.float32)

    def chunk_body(s, c, first):
        to = part.at[s % 2]
        lhs = a_buf.at[pick(STEPS[s]["lhs"]) * n_chunks + c]
        rhs = a_buf.at[pick(STEPS[s]["rhs"]) * n_chunks + c]
        parts = [(0, lhs[...], rhs[:TILE])]
        if STEPS[s]["diag"]:
            parts.append((BLK, lhs[TILE:], rhs[TILE:]))
        else:
            parts.append((BLK, lhs[...], rhs[TILE:]))
        for at, left, right in parts:
            n = left.shape[0]
            value = dot(left, right)
            to[at:at + n] = value if first else to[at:at + n] + value

    def chunks(s, lo, hi, wait_load):
        if hi - lo == 1:
            last = lo == n_chunks - 1
            if wait_load and not last:
                load(NEEDS[s], lo + 1).wait()
            chunk_body(s, lo, lo == 0)
            if s == 3:
                load(3, lo).start()
            return

        @pl.loop(lo, hi)
        def _(c):
            if wait_load:
                load(NEEDS[s], c + 1).wait()
            chunk_body(s, c, False)
            if s == 3:
                load(3, c).start()

    load(0, 0).wait()
    for s in range(len(STEPS)):
        fresh = s in NEEDS
        if s == 5:
            for c in range(n_chunks):
                load(4, c).start()
        chunks(s, 0, 1, fresh)
        chunks(s, 1, 3, fresh)
        if s == 0:
            pl.semaphore_wait(barrier, 3)
        else:
            reduce_step(s - 1)
        if s + 1 in NEEDS:
            load(NEEDS[s + 1], 0).wait()
        chunks(s, 3, n_chunks - 1, fresh)
        if s > 0:
            send_step(s - 1)
        chunks(s, n_chunks - 1, n_chunks, fresh)
        after_pop(s)

    reduce_step(len(STEPS) - 1)

    for slot in range(3):
        rows = DIAG if slot == 0 else FULL

        def finish(slot=slot, rows=rows):
            for half_id in range(2):
                link_wait(slot, half_id, rows // 2)

            @pl.loop(0, rows // 128)
            def _(i):
                to = pl.ds(pl.multiple_of(i * 128, 128), 128)
                own[slot, to] += recv[slot, to]

        if slot < 2:
            finish()
        else:
            pl.when(chip == 0)(finish)

            @pl.when(chip == 1)
            def _():
                own[2] = jnp.zeros((FULL, TILE), jnp.float32)

    own[0, DIAG:FULL] = own[0, TILE:2 * TILE].T

    def out_copy(slot, at, n, row, col, sem):
        return pltpu.make_async_copy(
            own.at[slot, pl.ds(at, n)], out_ref.at[0, slot, pl.ds(row, n), pl.ds(col, TILE)], out_sem.at[sem]
        )

    copies = [
        out_copy(0, 0, BLK, 0, 0, 0),
        out_copy(0, BLK, TILE, TILE, TILE, 1),
        out_copy(0, DIAG, TILE, 0, TILE, 2),
        out_copy(1, 0, BLK, 0, 0, 3),
        out_copy(1, BLK, BLK, 0, TILE, 4),
        out_copy(2, 0, BLK, 0, 0, 5),
        out_copy(2, BLK, BLK, 0, TILE, 6),
    ]
    for copy in copies:
        copy.start()
    for s in range(N_REMOTE):
        by_mode(s, lambda s=s: link_copy(s).wait_send(), lambda: None)
    for copy in copies:
        copy.wait()


def solution(mesh):
    groups = mesh.shape["dp"]
    assert groups == 4

    def local_gram(a_local):
        n_rows, local_cols = a_local.shape
        assert n_rows == groups * BLK and local_cols % CHUNK == 0
        n_chunks = local_cols // CHUNK
        return pl.pallas_call(
            kernel,
            name="gram",
            out_shape=jax.ShapeDtypeStruct((1, 3, BLK, BLK), jnp.float32),
            in_specs=[pl.BlockSpec(memory_space=pltpu.HBM)],
            out_specs=pl.BlockSpec(memory_space=pltpu.HBM),
            scratch_shapes=[
                pltpu.VMEM((3 * n_chunks, BLK, CHUNK), jnp.bfloat16),
                pltpu.VMEM((2, FULL, TILE), jnp.float32),
                pltpu.VMEM((N_REMOTE, FULL // 2, TILE), jnp.float32),
                pltpu.VMEM((3, FULL, TILE), jnp.float32),
                pltpu.VMEM((3, FULL, TILE), jnp.float32),
                pltpu.SemaphoreType.DMA((len(LOADS) * n_chunks,)),
                pltpu.SemaphoreType.DMA((len(STEPS),)),
                pltpu.SemaphoreType.DMA((len(STEPS),)),
                pltpu.SemaphoreType.DMA((N_REMOTE,)),
                pltpu.SemaphoreType.DMA((6,)),
                pltpu.SemaphoreType.DMA((7,)),
            ],
            compiler_params=pltpu.CompilerParams(
                collective_id=0, has_side_effects=True, vmem_limit_bytes=67043328
            ),
        )(a_local)

    return jax.shard_map(
        local_gram, mesh=mesh, in_specs=(P("mat", "dp"),), out_specs=P(("mat", "dp")), check_vma=False
    )
```

time: 376 us -> 110 us (0.29)
  matrix products: 146 us -> 0 us
  other arithmetic: 107 us -> 0 us
  Pallas kernels: 0 us -> 105 us
  waiting for transfers between devices: 92.3 us -> 0 us
  between operations: 13.4 us -> 0.01 us
  local copies, waits for them, and re-layouts: 15.7 us -> 3.86 us
    dot_general x3 -> x0, matrix products: 146 us -> none  [slot_step(): jnp.einsum('gik,gjk->gij', blocks, partner, preferred_element_type=jnp.fl...]
    pallas_call x0 -> x1, Pallas kernels: none -> 105 us  [local_gram(): pl.pallas_call(kernel, name='gram', out_shape=jax.ShapeDtypeStruct((1, 3,...]
    unnamed x2 -> x0, waiting for transfers between devices: 92.3 us -> none
    concatenate x1 -> x0, other arithmetic: 87.4 us -> none  [packed_partial(): doubled = jnp.concatenate([blocks, blocks], axis=0)]
    dynamic_update_slice x3 -> x0, other arithmetic: 19.7 us -> none  [slot_step(): lax.dynamic_update_index_in_dim(packed, jnp.where(keep_mask, flipped, 0.0...]
    dot_general x3 -> x0, local copies, waits for them, and re-layouts: 15.7 us -> none  [slot_step(): jnp.einsum('gik,gjk->gij', blocks, partner, preferred_element_type=jnp.fl...]
    unnamed x0 -> x1, local copies, waits for them, and re-layouts: none -> 3.86 us
  transfers between devices with their start and end apart: 1 -> 0, of which waited for: 1 -> 0; matrix products, arithmetic and copies ran while one was open for 0% -> 0% of each run, Pallas kernels for 0% -> 0%
where the time goes in v1:
time: 110 us; the launch traced here: 109 us
  Pallas kernels  105 us (95%)
  local copies, waits for them, and re-layouts  3.86 us (4%)
    pallas_call x1, Pallas kernels, local_gram(): pl.pallas_call(kernel, name='gram', out_shape=jax.ShapeDtypeStruct((1, 3,...  105 us
    unnamed x1, local copies, waits for them, and re-layouts  3.86 us

profile of v1, /device:TPU:1, one launch (start us, length us, event | category | flops | bytes accessed | tf_op | source)
XLA Modules:
  0.0 109.3 jit_solution(11011735691558798913)
XLA Ops:
  0.0 105.4 %gram.1 = f32[1,3,512,512]{3,2,1,0:T(8,128)} custom-call(bf16[2048,16384]{1,0:T(8,128)(2,1)} %a_ref.1), custom_call_target="tpu_custom_call" | custom-call | tf_op jit(solution)/shard_map/gram/pallas_call | solution.py:267
  105.4 3.9 %copy.3 = f32[1,3,512,512]{3,2,1,0:T(8,128)} copy(f32[1,3,512,512]{3,2,1,0:T(8,128)} %gram.1) | data formatting | bytes 6291456

commit v2 on v0

v2 whole, which is shorter than its diff:
```python
import jax
import jax.numpy as jnp
from jax import lax
from jax.experimental import pallas as pl
from jax.experimental.pallas import tpu as pltpu
from jax.sharding import PartitionSpec as P

BLK = 512
TILE = 256
DHALF = 3 * TILE // 2
MESH = pl.DeviceIdType.MESH

LHS = ((0, 1, 0, 1, 0, 1, 0, 1, 2, 0), (0, 1, 2, 1, 2, 2, 2, 0, 2, 0))
RHS = ((0, 0, 2, 1, 2, 2, 2, 0, 2, 0), (0, 0, 0, 1, 0, 1, 0, 1, 2, 0))
REMOTE = ((1, 1, 1, 1, 0, 0, 0, 0, 0, 0), (1, 1, 1, 1, 1, 1, 0, 0, 0, 0))
OWNER = ((0, 1, 0, 1, 0, 0, 1, 1, 0, 1), (0, 1, 0, 1, 0, 1, 1, 0, 1, 0))
SLOT = ((0, 1, 1, 0, 2, 1, 1, 2, 0, 0), (0, 1, 2, 0, 1, 2, 1, 1, 0, 0))
DIAG = tuple(int(a == b) for a, b in zip(LHS[0], RHS[0]))
N_STEPS = len(DIAG)
LAST = N_STEPS - 1
N_REMOTE = 6
LOADS = (((2, 0), 0), ((3, 1), 1), ((1, 2), 2), ((0, 3), 2), ((1, 2), 0))
FIRST = ((0, 1024), (1024, 2048), (2048, 4096), (4096, 8192), (8192, 12288), (12288, 16384))


def dot(lhs, rhs):
    return lax.dot_general(lhs, rhs, (((1,), (1,)), ((), ())), preferred_element_type=jnp.float32)


def gram_kernel(a_ref, own, a_buf, part, pair, recv, load_sem, d2d_send, d2d_recv, ici_send, ici_recv):
    half_cols = a_ref.shape[1] // 2
    me = lax.axis_index("dp")
    chip = me // 2
    core = me % 2
    peer = chip * 2 + (1 - core)

    def pick(two):
        return two[0] if two[0] == two[1] else two[0] * (1 - chip) + two[1] * chip

    def at(table, s):
        if isinstance(s, int):
            return pick((table[0][s], table[1][s]))
        packed = [sum(v << (2 * i) for i, v in enumerate(row)) for row in table]
        return (pick(packed) >> (2 * s)) & 3

    def load(which, lo, hi, sem):
        block, slot = LOADS[which]
        half = lo // half_cols
        return pltpu.make_async_copy(
            a_ref.at[pl.ds(pl.multiple_of(pick(block) * BLK, BLK), BLK), pl.ds(lo, hi - lo)],
            a_buf.at[slot * 2 + half, :, pl.ds(lo - half * half_cols, hi - lo)],
            load_sem.at[sem],
        )

    first_loads = [load(0, lo, hi, i) for i, (lo, hi) in enumerate(FIRST)]
    half_loads = [
        [load(which, h * half_cols, (h + 1) * half_cols, len(FIRST) + 2 * which + h) for h in range(2)]
        for which in range(1, len(LOADS))
    ]
    for copy in first_loads + half_loads[0] + half_loads[1]:
        copy.start()

    barrier = pltpu.get_barrier_semaphore()
    for hop in range(1, 4):
        pl.semaphore_signal(barrier, inc=1, device_id={"dp": (me + hop) % 4}, device_id_type=MESH)

    part[...] = jnp.zeros_like(part)

    @pl.when(chip == 1)
    def _():
        own[2] = jnp.zeros((2, BLK, TILE), jnp.float32)

    def pair_copy(s):
        return pltpu.make_async_remote_copy(
            src_ref=part.at[s % 2, 1 - core],
            dst_ref=pair.at[s],
            send_sem=d2d_send.at[s],
            recv_sem=d2d_recv.at[s],
            device_id={"dp": peer},
            device_id_type=MESH,
        )

    def own_copy(s, rows):
        return pltpu.make_async_remote_copy(
            src_ref=part.at[s % 2, :, pl.ds(0, rows)],
            dst_ref=own.at[at(SLOT, s), :, pl.ds(0, rows)],
            send_sem=d2d_send.at[s],
            recv_sem=d2d_recv.at[s],
            device_id={"dp": peer},
            device_id_type=MESH,
        )

    def link_copy(s, rows):
        slot = at(SLOT, s)
        return pltpu.make_async_remote_copy(
            src_ref=pair.at[s, pl.ds(0, rows)],
            dst_ref=recv.at[slot, core, pl.ds(0, rows)],
            send_sem=ici_send.at[s],
            recv_sem=ici_recv.at[slot * 2 + core],
            device_id={"dp": (1 - chip) * 2 + at(OWNER, s)},
            device_id_type=MESH,
        )

    def link_wait(slot, half, rows):
        pltpu.make_async_remote_copy(
            src_ref=pair.at[0, pl.ds(0, rows)],
            dst_ref=recv.at[slot, half, pl.ds(0, rows)],
            send_sem=ici_send.at[0],
            recv_sem=ici_recv.at[slot * 2 + half],
            device_id={"dp": peer},
            device_id_type=MESH,
        ).wait_recv()

    def on(value, want=1):
        return pl.when(value == want)

    def send_partial(s):
        @on(at(REMOTE, s))
        def _():
            pair_copy(s).start()

        @on(at(REMOTE, s) * 2 + (at(OWNER, s) + core) % 2)
        def _():
            own_copy(s, BLK).start()

    def reduce_partial(s):
        @on(at(REMOTE, s))
        def _():
            pair_copy(s).wait()

            @pl.loop(0, BLK // 64)
            def _(i):
                rows = pl.ds(pl.multiple_of(i * 64, 64), 64)
                pair[s, rows] += part[s % 2, core, rows]

            for diag, rows in ((1, DHALF), (0, BLK)):
                @on(at((DIAG, DIAG), s), diag)
                def _(rows=rows):
                    link_copy(s, rows).start()

        mine = at(REMOTE, s) * 2 + (at(OWNER, s) + core) % 2

        @on(mine, 0)
        def _():
            own_copy(s, BLK).wait_recv()
            slot = at(SLOT, s)

            @pl.loop(0, BLK // 64)
            def _(i):
                rows = pl.ds(pl.multiple_of(i * 64, 64), 64)
                for h in range(2):
                    own[slot, h, rows] += part[s % 2, h, rows]

        @on(mine, 1)
        def _():
            own_copy(s, BLK).wait_send()

    def put_diag(to, low, high, add):
        for h, row, n, value in (
            (0, 0, DHALF, low[:DHALF]),
            (1, 0, BLK - DHALF, low[DHALF:]),
            (1, BLK - DHALF, TILE, high),
        ):
            to[h, row:row + n] = to[h, row:row + n] + value if add else value

    for i, (lo, hi) in enumerate(FIRST):
        first_loads[i].wait()
        half = lo // half_cols
        cols = slice(lo - half * half_cols, hi - half * half_cols)
        block = a_buf.at[half, :, cols]
        put_diag(part.at[0], dot(block[...], block[:TILE]), dot(block[TILE:], block[TILE:]), i > 0)
    pl.semaphore_wait(barrier, 3)
    send_partial(0)

    @pl.loop(1, 3)
    def _(s):
        @pl.loop(0, 2)
        def _(h):
            @on(s * 2 + h, 2)
            def _():
                half_loads[0][0].wait()

            @on(s * 2 + h, 3)
            def _():
                half_loads[0][1].wait()

            @on(s * 2 + h, 4)
            def _():
                half_loads[1][0].wait()
                half_loads[1][1].wait()

            @on(h)
            def _():
                reduce_partial(s - 1)

            value = dot(a_buf[at(LHS, s) * 2 + h], a_buf[at(RHS, s) * 2 + h])
            for n in range(2):
                old = jnp.where(h == 0, 0.0, part[s % 2, n])
                part[s % 2, n] = old + value[:, n * TILE:(n + 1) * TILE]

        send_partial(s)

    @pl.loop(3, N_STEPS)
    def _(s):
        for step, copies, action in (
            (3, half_loads[2], "start"),
            (4, half_loads[2], "wait"),
            (5, half_loads[3], "start"),
            (6, half_loads[3], "wait"),
        ):
            @on(s, step)
            def _(copies=copies, action=action):
                for copy in copies:
                    getattr(copy, action)()

        diag = at((DIAG, DIAG), s)
        to = part.at[s % 2]
        left, right = at(LHS, s) * 2, at(RHS, s) * 2

        @on(diag)
        def _():
            for h in range(2):
                block = a_buf.at[left + h]
                put_diag(to, dot(block[...], block[:TILE]), dot(block[TILE:], block[TILE:]), h > 0)

        @on(diag, 0)
        def _():
            for h in range(2):
                value = dot(a_buf[left + h], a_buf[right + h])
                for n in range(2):
                    tile = value[:, n * TILE:(n + 1) * TILE]
                    to[n] = to[n] + tile if h else tile

        reduce_partial(s - 1)

        @pl.when(s < LAST)
        def _():
            send_partial(s)

    mine = at(OWNER, LAST) == core
    pl.when(jnp.logical_not(mine))(lambda: own_copy(LAST, DHALF).start())

    def add_link(slot, rows):
        for h in range(2):
            link_wait(slot, h, rows)

        @pl.loop(0, rows // 64)
        def _(i):
            to = pl.ds(pl.multiple_of(i * 64, 64), 64)
            for h in range(2):
                own[slot, h, to] += recv[slot, h, to]

    add_link(1, BLK)
    pl.when(chip == 0)(lambda: add_link(2, BLK))

    @pl.when(mine)
    def _():
        for h in range(2):
            link_wait(0, h, DHALF)

        @pl.loop(0, DHALF // 64)
        def _(i):
            to = pl.ds(pl.multiple_of(i * 64, 64), 64)
            for h in range(2):
                part[LAST % 2, h, to] += recv[0, h, to]

        own_copy(LAST, DHALF).wait_recv()

        @pl.loop(0, DHALF // 64)
        def _(i):
            to = pl.ds(pl.multiple_of(i * 64, 64), 64)
            for h in range(2):
                own[0, h, to] += part[LAST % 2, h, to]

    @pl.when(jnp.logical_not(mine))
    def _():
        add_link(0, DHALF)
        own_copy(LAST, DHALF).wait_send()

    low = jnp.concatenate([own[0, 0, TILE:DHALF], own[0, 1, :BLK - DHALF]], axis=0)
    flipped = low.T
    own[0, 0, DHALF:] = flipped[:BLK - DHALF]
    own[0, 1, DHALF:] = flipped[BLK - DHALF:]

    for s in range(N_REMOTE):
        rows = DHALF if DIAG[s] else BLK

        @on(at(REMOTE, s))
        def _(s=s, rows=rows):
            link_copy(s, rows).wait_send()


def place_kernel(own, out_ref, sem):
    rest = BLK - DHALF
    moves = [
        (0, 0, 0, DHALF, 0, 0),
        (0, 1, 0, rest, DHALF, 0),
        (0, 1, rest, TILE, TILE, TILE),
        (0, 0, DHALF, rest, 0, TILE),
        (0, 1, DHALF, rest, rest, TILE),
    ] + [(slot, h, 0, BLK, 0, h * TILE) for slot in (1, 2) for h in range(2)]
    copies = [
        pltpu.make_async_copy(
            own.at[slot, h, pl.ds(src, n)], out_ref.at[0, slot, pl.ds(row, n), pl.ds(col, TILE)], sem.at[i]
        )
        for i, (slot, h, src, n, row, col) in enumerate(moves)
    ]
    for copy in copies:
        copy.start()
    for copy in copies:
        copy.wait()


def solution(mesh):
    groups = mesh.shape["dp"]
    assert groups == 4

    def local_gram(a_local):
        n_rows, local_cols = a_local.shape
        assert n_rows == groups * BLK and local_cols == FIRST[-1][1]
        own = pl.pallas_call(
            gram_kernel,
            name="gram",
            out_shape=pltpu.VMEM((3, 2, BLK, TILE), jnp.float32),
            in_specs=[pl.BlockSpec(memory_space=pltpu.HBM)],
            out_specs=pl.BlockSpec(memory_space=pltpu.VMEM),
            scratch_shapes=[
                pltpu.VMEM((6, BLK, local_cols // 2), jnp.bfloat16),
                pltpu.VMEM((2, 2, BLK, TILE), jnp.float32),
                pltpu.VMEM((N_REMOTE, BLK, TILE), jnp.float32),
                pltpu.VMEM((3, 2, BLK, TILE), jnp.float32),
                pltpu.SemaphoreType.DMA((len(FIRST) + 2 * len(LOADS),)),
                pltpu.SemaphoreType.DMA((N_STEPS,)),
                pltpu.SemaphoreType.DMA((N_STEPS,)),
                pltpu.SemaphoreType.DMA((N_REMOTE,)),
                pltpu.SemaphoreType.DMA((6,)),
            ],
            compiler_params=pltpu.CompilerParams(
                collective_id=0, has_side_effects=True, vmem_limit_bytes=58 * 2**20
            ),
        )(a_local)
        return pl.pallas_call(
            place_kernel,
            name="place",
            out_shape=jax.ShapeDtypeStruct((1, 3, BLK, BLK), jnp.float32),
            in_specs=[pl.BlockSpec(memory_space=pltpu.VMEM)],
            out_specs=pl.BlockSpec(memory_space=pltpu.HBM),
            scratch_shapes=[pltpu.SemaphoreType.DMA((9,))],
        )(pltpu.with_memory_space_constraint(own, pltpu.VMEM))

    return jax.shard_map(
        local_gram, mesh=mesh, in_specs=(P("mat", "dp"),), out_specs=P(("mat", "dp")), check_vma=False
    )
```

time: 376 us -> 91.6 us (0.24)
  matrix products: 146 us -> 0 us
  other arithmetic: 107 us -> 0 us
  waiting for transfers between devices: 92.3 us -> 0 us
  Pallas kernels: 0 us -> 90.4 us
  local copies, waits for them, and re-layouts: 15.7 us -> 0 us
  between operations: 13.4 us -> 0.17 us
    dot_general x3 -> x0, matrix products: 146 us -> none  [slot_step(): jnp.einsum('gik,gjk->gij', blocks, partner, preferred_element_type=jnp.fl...]
    unnamed x2 -> x0, waiting for transfers between devices: 92.3 us -> none
    pallas_call x0 -> x2, Pallas kernels: none -> 90.4 us  [the longest x1 88.6 us: local_gram(): pl.pallas_call(gram_kernel, name='gram', out_shape=pltpu.VMEM((3, 2, BLK,...]
    concatenate x1 -> x0, other arithmetic: 87.4 us -> none  [packed_partial(): doubled = jnp.concatenate([blocks, blocks], axis=0)]
    dynamic_update_slice x3 -> x0, other arithmetic: 19.7 us -> none  [slot_step(): lax.dynamic_update_index_in_dim(packed, jnp.where(keep_mask, flipped, 0.0...]
    dot_general x3 -> x0, local copies, waits for them, and re-layouts: 15.7 us -> none  [slot_step(): jnp.einsum('gik,gjk->gij', blocks, partner, preferred_element_type=jnp.fl...]
  transfers between devices with their start and end apart: 1 -> 0, of which waited for: 1 -> 0; matrix products, arithmetic and copies ran while one was open for 0% -> 0% of each run, Pallas kernels for 0% -> 0%
where the time goes in v2:
time: 91.6 us; the launch traced here: 90.5 us
  Pallas kernels  90.4 us (99%)
    pallas_call x1, Pallas kernels, local_gram(): pl.pallas_call(gram_kernel, name='gram', out_shape=pltpu.VMEM((3, 2, BLK,...  88.6 us

profile of v2, /device:TPU:1, one launch (start us, length us, event | category | flops | bytes accessed | tf_op | source)
XLA Modules:
  0.0 90.5 jit_solution(7310291491938311327)
XLA Ops:
  0.0 88.6 %gram.1.own = f32[3,2,512,256]{3,2,1,0:T(8,128)S(1)} custom-call(bf16[2048,16384]{1,0:T(8,128)(2,1)} %a_ref.1), custom_call_target="tpu_custom_call" | custom-call | tf_op jit(solution)/shard_map/gram/pallas_call | solution.py:321
  88.6 1.7 %place.1 = f32[1,3,512,512]{3,2,1,0:T(8,128)} custom-call(f32[3,2,512,256]{3,2,1,0:T(8,128)S(1)} %gram.1.own), custom_call_target="tpu_custom_call" | custom-call | tf_op jit(solution)/shard_map/place/pallas_call | solution.py:342

commit v3 on v2

--- a/solution.py
+++ b/solution.py
@@ -10,17 +10,18 @@
 DHALF = 3 * TILE // 2
 MESH = pl.DeviceIdType.MESH
 
-LHS = ((0, 1, 0, 1, 0, 1, 0, 1, 2, 0), (0, 1, 2, 1, 2, 2, 2, 0, 2, 0))
-RHS = ((0, 0, 2, 1, 2, 2, 2, 0, 2, 0), (0, 0, 0, 1, 0, 1, 0, 1, 2, 0))
+LHS = ((0, 1, 0, 1, 0, 1, 0, 1, 0, 0), (0, 1, 2, 1, 2, 2, 2, 0, 0, 0))
+RHS = ((0, 0, 2, 1, 2, 2, 2, 0, 0, 0), (0, 0, 0, 1, 0, 1, 0, 1, 0, 0))
 REMOTE = ((1, 1, 1, 1, 0, 0, 0, 0, 0, 0), (1, 1, 1, 1, 1, 1, 0, 0, 0, 0))
-OWNER = ((0, 1, 0, 1, 0, 0, 1, 1, 0, 1), (0, 1, 0, 1, 0, 1, 1, 0, 1, 0))
+OWNER = ((0, 1, 0, 1, 0, 0, 1, 1, 0, 0), (0, 1, 0, 1, 0, 1, 1, 0, 0, 0))
 SLOT = ((0, 1, 1, 0, 2, 1, 1, 2, 0, 0), (0, 1, 2, 0, 1, 2, 1, 1, 0, 0))
 DIAG = tuple(int(a == b) for a, b in zip(LHS[0], RHS[0]))
 N_STEPS = len(DIAG)
 LAST = N_STEPS - 1
 N_REMOTE = 6
 LOADS = (((2, 0), 0), ((3, 1), 1), ((1, 2), 2), ((0, 3), 2), ((1, 2), 0))
-FIRST = ((0, 1024), (1024, 2048), (2048, 4096), (4096, 8192), (8192, 12288), (12288, 16384))
+FIRST = (((0, 1024),), ((1024, 2816),), ((2816, 5888),), ((5888, 8192), (8192, 10496)), ((10496, 16384),))
+FIRST_LOADS = sum(FIRST, ())
 
 
 def dot(lhs, rhs):
@@ -42,6 +43,10 @@
             return pick((table[0][s], table[1][s]))
         packed = [sum(v << (2 * i) for i, v in enumerate(row)) for row in table]
         return (pick(packed) >> (2 * s)) & 3
+
+    def operand(table, s):
+        last_slots = 2 * ((chip + core + LAST - s) % 2)
+        return jnp.where(s < LAST - 1, at(table, s), 0) + jnp.where(s < LAST - 1, 0, 1) * (2 - last_slots)
 
     def load(which, lo, hi, sem):
         block, slot = LOADS[which]
@@ -52,9 +57,9 @@
             load_sem.at[sem],
         )
 
-    first_loads = [load(0, lo, hi, i) for i, (lo, hi) in enumerate(FIRST)]
+    first_loads = [load(0, lo, hi, i) for i, (lo, hi) in enumerate(FIRST_LOADS)]
     half_loads = [
-        [load(which, h * half_cols, (h + 1) * half_cols, len(FIRST) + 2 * which + h) for h in range(2)]
+        [load(which, h * half_cols, (h + 1) * half_cols, len(FIRST_LOADS) + 2 * which + h) for h in range(2)]
         for which in range(1, len(LOADS))
     ]
     for copy in first_loads + half_loads[0] + half_loads[1]:
@@ -119,7 +124,7 @@
         def _():
             pair_copy(s).start()
 
-        @on(at(REMOTE, s) * 2 + (at(OWNER, s) + core) % 2)
+        @on(jnp.where(s == LAST - 1, 1, at(REMOTE, s) * 2 + (at(OWNER, s) + core) % 2))
         def _():
             own_copy(s, BLK).start()
 
@@ -128,10 +133,7 @@
         def _():
             pair_copy(s).wait()
 
-            @pl.loop(0, BLK // 64)
-            def _(i):
-                rows = pl.ds(pl.multiple_of(i * 64, 64), 64)
-                pair[s, rows] += part[s % 2, core, rows]
+            pair[s] += part[s % 2, core]
 
             for diag, rows in ((1, DHALF), (0, BLK)):
                 @on(at((DIAG, DIAG), s), diag)
@@ -143,13 +145,7 @@
         @on(mine, 0)
         def _():
             own_copy(s, BLK).wait_recv()
-            slot = at(SLOT, s)
-
-            @pl.loop(0, BLK // 64)
-            def _(i):
-                rows = pl.ds(pl.multiple_of(i * 64, 64), 64)
-                for h in range(2):
-                    own[slot, h, rows] += part[s % 2, h, rows]
+            own[at(SLOT, s)] += part[s % 2]
 
         @on(mine, 1)
         def _():
@@ -163,12 +159,14 @@
         ):
             to[h, row:row + n] = to[h, row:row + n] + value if add else value
 
-    for i, (lo, hi) in enumerate(FIRST):
-        first_loads[i].wait()
-        half = lo // half_cols
-        cols = slice(lo - half * half_cols, hi - half * half_cols)
-        block = a_buf.at[half, :, cols]
-        put_diag(part.at[0], dot(block[...], block[:TILE]), dot(block[TILE:], block[TILE:]), i > 0)
+    arriving = iter(first_loads)
+    for i, piece in enumerate(FIRST):
+        for _ in piece:
+            next(arriving).wait()
+        for lo, hi in piece:
+            half = lo // half_cols
+            block = a_buf.at[half, :, lo - half * half_cols:hi - half * half_cols]
+            put_diag(part.at[0], dot(block[...], block[:TILE]), dot(block[TILE:], block[TILE:]), lo > 0)
     pl.semaphore_wait(barrier, 3)
     send_partial(0)
 
@@ -193,7 +191,7 @@
             def _():
                 reduce_partial(s - 1)
 
-            value = dot(a_buf[at(LHS, s) * 2 + h], a_buf[at(RHS, s) * 2 + h])
+            value = dot(a_buf[operand(LHS, s) * 2 + h], a_buf[operand(RHS, s) * 2 + h])
             for n in range(2):
                 old = jnp.where(h == 0, 0.0, part[s % 2, n])
                 part[s % 2, n] = old + value[:, n * TILE:(n + 1) * TILE]
@@ -215,7 +213,7 @@
 
         diag = at((DIAG, DIAG), s)
         to = part.at[s % 2]
-        left, right = at(LHS, s) * 2, at(RHS, s) * 2
+        left, right = operand(LHS, s) * 2, operand(RHS, s) * 2
 
         @on(diag)
         def _():
@@ -231,51 +229,24 @@
                     tile = value[:, n * TILE:(n + 1) * TILE]
                     to[n] = to[n] + tile if h else tile
 
-        reduce_partial(s - 1)
-
         @pl.when(s < LAST)
         def _():
+            reduce_partial(s - 1)
             send_partial(s)
 
-    mine = at(OWNER, LAST) == core
-    pl.when(jnp.logical_not(mine))(lambda: own_copy(LAST, DHALF).start())
-
-    def add_link(slot, rows):
+    for h in range(2):
+        link_wait(0, h, DHALF)
+    own_copy(LAST - 1, BLK).wait()
+    for h in range(2):
+        own[0, h, :DHALF] += part[LAST % 2, h, :DHALF] + recv[0, h, :DHALF]
+
+    def add_link(slot):
         for h in range(2):
-            link_wait(slot, h, rows)
-
-        @pl.loop(0, rows // 64)
-        def _(i):
-            to = pl.ds(pl.multiple_of(i * 64, 64), 64)
-            for h in range(2):
-                own[slot, h, to] += recv[slot, h, to]
-
-    add_link(1, BLK)
-    pl.when(chip == 0)(lambda: add_link(2, BLK))
-
-    @pl.when(mine)
-    def _():
-        for h in range(2):
-            link_wait(0, h, DHALF)
-
-        @pl.loop(0, DHALF // 64)
-        def _(i):
-            to = pl.ds(pl.multiple_of(i * 64, 64), 64)
-            for h in range(2):
-                part[LAST % 2, h, to] += recv[0, h, to]
-
-        own_copy(LAST, DHALF).wait_recv()
-
-        @pl.loop(0, DHALF // 64)
-        def _(i):
-            to = pl.ds(pl.multiple_of(i * 64, 64), 64)
-            for h in range(2):
-                own[0, h, to] += part[LAST % 2, h, to]
-
-    @pl.when(jnp.logical_not(mine))
-    def _():
-        add_link(0, DHALF)
-        own_copy(LAST, DHALF).wait_send()
+            link_wait(slot, h, BLK)
+        own[slot] += recv[slot]
+
+    add_link(1)
+    pl.when(chip == 0)(lambda: add_link(2))
 
     low = jnp.concatenate([own[0, 0, TILE:DHALF], own[0, 1, :BLK - DHALF]], axis=0)
     flipped = low.T
@@ -317,7 +288,7 @@
 
     def local_gram(a_local):
         n_rows, local_cols = a_local.shape
-        assert n_rows == groups * BLK and local_cols == FIRST[-1][1]
+        assert n_rows == groups * BLK and local_cols == FIRST_LOADS[-1][1]
         own = pl.pallas_call(
             gram_kernel,
             name="gram",
@@ -329,14 +300,14 @@
                 pltpu.VMEM((2, 2, BLK, TILE), jnp.float32),
                 pltpu.VMEM((N_REMOTE, BLK, TILE), jnp.float32),
                 pltpu.VMEM((3, 2, BLK, TILE), jnp.float32),
-                pltpu.SemaphoreType.DMA((len(FIRST) + 2 * len(LOADS),)),
+                pltpu.SemaphoreType.DMA((len(FIRST_LOADS) + 2 * len(LOADS),)),
                 pltpu.SemaphoreType.DMA((N_STEPS,)),
                 pltpu.SemaphoreType.DMA((N_STEPS,)),
                 pltpu.SemaphoreType.DMA((N_REMOTE,)),
                 pltpu.SemaphoreType.DMA((6,)),
             ],
             compiler_params=pltpu.CompilerParams(
-                collective_id=0, has_side_effects=True, vmem_limit_bytes=58 * 2**20
+                collective_id=0, has_side_effects=True, vmem_limit_bytes=60 * 2**20
             ),
         )(a_local)
         return pl.pallas_call(

time: 91.6 us -> 88.5 us (0.966); the launches traced: 90.5 us -> 88.4 us
  Pallas kernels: 90.4 us -> 88.2 us
    pallas_call x1, Pallas kernels: 88.6 us -> 86.5 us  [local_gram(): pl.pallas_call(gram_kernel, name='gram', out_shape=pltpu.VMEM((3, 2, BLK,...]
where the time goes in v3:
time: 88.5 us; the launch traced here: 88.4 us
  Pallas kernels  88.2 us (100%)
    pallas_call x1, Pallas kernels, local_gram(): pl.pallas_call(gram_kernel, name='gram', out_shape=pltpu.VMEM((3, 2, BLK,...  86.5 us

profile of v3, /device:TPU:1, one launch (start us, length us, event | category | flops | bytes accessed | tf_op | source)
XLA Modules:
  0.0 88.4 jit_solution(14377291113931077319)
XLA Ops:
  0.0 86.5 %gram.1.own = f32[3,2,512,256]{3,2,1,0:T(8,128)S(1)} custom-call(bf16[2048,16384]{1,0:T(8,128)(2,1)} %a_ref.1), custom_call_target="tpu_custom_call" | custom-call | tf_op jit(solution)/shard_map/gram/pallas_call | solution.py:292
  86.5 1.7 %place.1 = f32[1,3,512,512]{3,2,1,0:T(8,128)} custom-call(f32[3,2,512,256]{3,2,1,0:T(8,128)S(1)} %gram.1.own), custom_call_target="tpu_custom_call" | custom-call | tf_op jit(solution)/shard_map/place/pallas_call | solution.py:313

commit v4 on v3

--- a/solution.py
+++ b/solution.py
@@ -20,7 +20,7 @@
 LAST = N_STEPS - 1
 N_REMOTE = 6
 LOADS = (((2, 0), 0), ((3, 1), 1), ((1, 2), 2), ((0, 3), 2), ((1, 2), 0))
-FIRST = (((0, 1024),), ((1024, 2816),), ((2816, 5888),), ((5888, 8192), (8192, 10496)), ((10496, 16384),))
+FIRST = (((0, 1024),), ((1024, 3072),), ((3072, 7168),), ((7168, 8192), (8192, 12288)), ((12288, 16384),))
 FIRST_LOADS = sum(FIRST, ())
 
 
@@ -28,7 +28,7 @@
     return lax.dot_general(lhs, rhs, (((1,), (1,)), ((), ())), preferred_element_type=jnp.float32)
 
 
-def gram_kernel(a_ref, own, a_buf, part, pair, recv, load_sem, d2d_send, d2d_recv, ici_send, ici_recv):
+def gram_kernel(a_ref, own, part, recv, a_buf, pair, load_sem, d2d_send, d2d_recv, ici_send, ici_recv):
     half_cols = a_ref.shape[1] // 2
     me = lax.axis_index("dp")
     chip = me // 2
@@ -70,10 +70,6 @@
         pl.semaphore_signal(barrier, inc=1, device_id={"dp": (me + hop) % 4}, device_id_type=MESH)
 
     part[...] = jnp.zeros_like(part)
-
-    @pl.when(chip == 1)
-    def _():
-        own[2] = jnp.zeros((2, BLK, TILE), jnp.float32)
 
     def pair_copy(s):
         return pltpu.make_async_remote_copy(
@@ -170,7 +166,7 @@
     pl.semaphore_wait(barrier, 3)
     send_partial(0)
 
-    @pl.loop(1, 3)
+    @pl.loop(1, 2)
     def _(s):
         @pl.loop(0, 2)
         def _(h):
@@ -182,11 +178,6 @@
             def _():
                 half_loads[0][1].wait()
 
-            @on(s * 2 + h, 4)
-            def _():
-                half_loads[1][0].wait()
-                half_loads[1][1].wait()
-
             @on(h)
             def _():
                 reduce_partial(s - 1)
@@ -198,9 +189,10 @@
 
         send_partial(s)
 
-    @pl.loop(3, N_STEPS)
+    @pl.loop(2, N_STEPS)
     def _(s):
         for step, copies, action in (
+            (2, half_loads[1], "wait"),
             (3, half_loads[2], "start"),
             (4, half_loads[2], "wait"),
             (5, half_loads[3], "start"),
@@ -234,24 +226,15 @@
             reduce_partial(s - 1)
             send_partial(s)
 
+    own_copy(LAST - 1, BLK).wait()
     for h in range(2):
         link_wait(0, h, DHALF)
-    own_copy(LAST - 1, BLK).wait()
-    for h in range(2):
-        own[0, h, :DHALF] += part[LAST % 2, h, :DHALF] + recv[0, h, :DHALF]
-
-    def add_link(slot):
+        link_wait(1, h, BLK)
+
+    @pl.when(chip == 0)
+    def _():
         for h in range(2):
-            link_wait(slot, h, BLK)
-        own[slot] += recv[slot]
-
-    add_link(1)
-    pl.when(chip == 0)(lambda: add_link(2))
-
-    low = jnp.concatenate([own[0, 0, TILE:DHALF], own[0, 1, :BLK - DHALF]], axis=0)
-    flipped = low.T
-    own[0, 0, DHALF:] = flipped[:BLK - DHALF]
-    own[0, 1, DHALF:] = flipped[BLK - DHALF:]
+            link_wait(2, h, BLK)
 
     for s in range(N_REMOTE):
         rows = DHALF if DIAG[s] else BLK
@@ -261,23 +244,42 @@
             link_copy(s, rows).wait_send()
 
 
-def place_kernel(own, out_ref, sem):
+def place_kernel(own, part, recv, out_ref, done, sem):
+    chip = lax.axis_index("dp") // 2
     rest = BLK - DHALF
-    moves = [
-        (0, 0, 0, DHALF, 0, 0),
-        (0, 1, 0, rest, DHALF, 0),
-        (0, 1, rest, TILE, TILE, TILE),
-        (0, 0, DHALF, rest, 0, TILE),
-        (0, 1, DHALF, rest, rest, TILE),
-    ] + [(slot, h, 0, BLK, 0, h * TILE) for slot in (1, 2) for h in range(2)]
-    copies = [
-        pltpu.make_async_copy(
-            own.at[slot, h, pl.ds(src, n)], out_ref.at[0, slot, pl.ds(row, n), pl.ds(col, TILE)], sem.at[i]
-        )
-        for i, (slot, h, src, n, row, col) in enumerate(moves)
-    ]
-    for copy in copies:
-        copy.start()
+    copies = []
+
+    def move(slot, h, src, n, row, col):
+        i = len(copies)
+        copies.append(
+            pltpu.make_async_copy(
+                done.at[slot, h, pl.ds(src, n)], out_ref.at[0, slot, pl.ds(row, n), pl.ds(col, TILE)], sem.at[i]
+            )
+        )
+        copies[i].start()
+
+    def diag_sum(h, row, n):
+        return own[0, h, row:row + n] + part[LAST % 2, h, row:row + n] + recv[0, h, row:row + n]
+
+    low = [diag_sum(0, TILE, DHALF - TILE), diag_sum(1, 0, rest)]
+    done[0, 0, TILE:DHALF] = low[0]
+    done[0, 1, :rest] = low[1]
+    done[0, 0, :TILE] = diag_sum(0, 0, TILE)
+    move(0, 0, 0, DHALF, 0, 0)
+    move(0, 1, 0, rest, DHALF, 0)
+    done[0, 1, rest:DHALF] = diag_sum(1, rest, TILE)
+    move(0, 1, rest, TILE, TILE, TILE)
+    flipped = jnp.concatenate(low, axis=0).T
+    done[0, 0, DHALF:] = flipped[:rest]
+    done[0, 1, DHALF:] = flipped[rest:]
+    move(0, 0, DHALF, rest, 0, TILE)
+    move(0, 1, DHALF, rest, rest, TILE)
+    for h in range(2):
+        done[1, h] = own[1, h] + recv[1, h]
+        move(1, h, 0, BLK, 0, h * TILE)
+    for h in range(2):
+        done[2, h] = jnp.where(chip == 0, own[2, h] + recv[2, h], 0.0)
+        move(2, h, 0, BLK, 0, h * TILE)
     for copy in copies:
         copy.wait()
 
@@ -289,17 +291,15 @@
     def local_gram(a_local):
         n_rows, local_cols = a_local.shape
         assert n_rows == groups * BLK and local_cols == FIRST_LOADS[-1][1]
-        own = pl.pallas_call(
+        sums = pl.pallas_call(
             gram_kernel,
             name="gram",
-            out_shape=pltpu.VMEM((3, 2, BLK, TILE), jnp.float32),
+            out_shape=[pltpu.VMEM((n, 2, BLK, TILE), jnp.float32) for n in (3, 2, 3)],
             in_specs=[pl.BlockSpec(memory_space=pltpu.HBM)],
-            out_specs=pl.BlockSpec(memory_space=pltpu.VMEM),
+            out_specs=[pl.BlockSpec(memory_space=pltpu.VMEM)] * 3,
             scratch_shapes=[
                 pltpu.VMEM((6, BLK, local_cols // 2), jnp.bfloat16),
-                pltpu.VMEM((2, 2, BLK, TILE), jnp.float32),
                 pltpu.VMEM((N_REMOTE, BLK, TILE), jnp.float32),
-                pltpu.VMEM((3, 2, BLK, TILE), jnp.float32),
                 pltpu.SemaphoreType.DMA((len(FIRST_LOADS) + 2 * len(LOADS),)),
                 pltpu.SemaphoreType.DMA((N_STEPS,)),
                 pltpu.SemaphoreType.DMA((N_STEPS,)),
@@ -307,17 +307,18 @@
                 pltpu.SemaphoreType.DMA((6,)),
             ],
             compiler_params=pltpu.CompilerParams(
-                collective_id=0, has_side_effects=True, vmem_limit_bytes=60 * 2**20
+                collective_id=0, has_side_effects=True, vmem_limit_bytes=55 * 2**20
             ),
         )(a_local)
         return pl.pallas_call(
             place_kernel,
             name="place",
             out_shape=jax.ShapeDtypeStruct((1, 3, BLK, BLK), jnp.float32),
-            in_specs=[pl.BlockSpec(memory_space=pltpu.VMEM)],
+            in_specs=[pl.BlockSpec(memory_space=pltpu.VMEM)] * 3,
             out_specs=pl.BlockSpec(memory_space=pltpu.HBM),
-            scratch_shapes=[pltpu.SemaphoreType.DMA((9,))],
-        )(pltpu.with_memory_space_constraint(own, pltpu.VMEM))
+            scratch_shapes=[pltpu.VMEM((3, 2, BLK, TILE), jnp.float32), pltpu.SemaphoreType.DMA((9,))],
+            compiler_params=pltpu.CompilerParams(vmem_limit_bytes=8 * 2**20),
+        )(*[pltpu.with_memory_space_constraint(x, pltpu.VMEM) for x in sums])
 
     return jax.shard_map(
         local_gram, mesh=mesh, in_specs=(P("mat", "dp"),), out_specs=P(("mat", "dp")), check_vma=False

time: 88.5 us -> 87.7 us (level)
  no operation moved by 1% of the time
where the time goes in v4:
time: 87.7 us
  Pallas kernels  87.5 us (100%)
    pallas_call x1, Pallas kernels, local_gram(): pl.pallas_call(gram_kernel, name='gram', out_shape=[pltpu.VMEM((n, 2, BLK...  85.7 us
    pallas_call x1, Pallas kernels, local_gram(): pl.pallas_call(place_kernel, name='place', out_shape=jax.ShapeDtypeStruct...  1.82 us

profile of v4, /device:TPU:1, one launch (start us, length us, event | category | flops | bytes accessed | tf_op | source)
XLA Modules:
  0.0 87.7 jit_solution(6640870636904918759)
XLA Ops:
  0.0 85.7 %gram.1 = (f32[3,2,512,256]{3,2,1,0:T(8,128)S(1)}, f32[2,2,512,256]{3,2,1,0:T(8,128)S(1)}, f32[3,2,512,256]{3,2,1,0:T(8,128)S(1)}) custom-call(bf16[2048,16384]{1,0:T(8,128)(2,1)} %a_ref.1), custom_call_target="tpu_custom_call" | custom-call | tf_op jit(solution)/shard_map/gram/pallas_call | solution.py:294
  85.7 1.8 %place.1 = f32[1,3,512,512]{3,2,1,0:T(8,128)} custom-call(f32[3,2,512,256]{3,2,1,0:T(8,128)S(1)} %get-tuple-element.8.own, f32[2,2,512,256]{3,2,1,0:T(8,128)S(1)} %get-tuple-element.9.part, f32[3,2,512,256]{3,2,1,0:T(8,128)S(1)} %get-tuple-element.10.recv), custom_call_target="tpu_custom_call" | custom-call | tf_op jit(solution)/shard_map/place/pallas_call | solution.py:313

commit v5 on v4

--- a/solution.py
+++ b/solution.py
@@ -20,9 +20,8 @@
 LAST = N_STEPS - 1
 N_REMOTE = 6
 LOADS = (((2, 0), 0), ((3, 1), 1), ((1, 2), 2), ((0, 3), 2), ((1, 2), 0))
-FIRST = (((0, 1024),), ((1024, 3072),), ((3072, 7168),), ((7168, 8192), (8192, 12288)), ((12288, 16384),))
-FIRST_LOADS = sum(FIRST, ())
-
+FIRST = ((2, 1024), (1, 2048), (3, 4096))
+N_FIRST = sum(n for n, _ in FIRST)
 
 def dot(lhs, rhs):
     return lax.dot_general(lhs, rhs, (((1,), (1,)), ((), ())), preferred_element_type=jnp.float32)
@@ -57,12 +56,33 @@
             load_sem.at[sem],
         )
 
-    first_loads = [load(0, lo, hi, i) for i, (lo, hi) in enumerate(FIRST_LOADS)]
+    def first_load(base, width, c):
+        col = pl.multiple_of(base + c * width, width)
+        cols = pl.ds(pl.multiple_of(col % half_cols, width), width)
+        return col // half_cols, cols, pl.ds(col, width)
+
+    segments = []
+    for n, width in FIRST:
+        done = sum(m for m, _, _ in segments)
+        base = sum(m * w for m, w, _ in segments)
+        segments.append((n, width, (base, done)))
+
+    def first_copy(width, start, c):
+        half, cols, src = first_load(start[0], width, c)
+        return pltpu.make_async_copy(
+            a_ref.at[pl.ds(pl.multiple_of(pick(LOADS[0][0]) * BLK, BLK), BLK), src],
+            a_buf.at[LOADS[0][1] * 2 + half, :, cols],
+            load_sem.at[start[1] + c],
+        )
+
     half_loads = [
-        [load(which, h * half_cols, (h + 1) * half_cols, len(FIRST_LOADS) + 2 * which + h) for h in range(2)]
+        [load(which, h * half_cols, (h + 1) * half_cols, N_FIRST + 2 * which + h) for h in range(2)]
         for which in range(1, len(LOADS))
     ]
-    for copy in first_loads + half_loads[0] + half_loads[1]:
+    for n, width, start in segments:
+        for c in range(n):
+            first_copy(width, start, c).start()
+    for copy in half_loads[0] + half_loads[1]:
         copy.start()
 
     barrier = pltpu.get_barrier_semaphore()
@@ -155,14 +175,14 @@
         ):
             to[h, row:row + n] = to[h, row:row + n] + value if add else value
 
-    arriving = iter(first_loads)
-    for i, piece in enumerate(FIRST):
-        for _ in piece:
-            next(arriving).wait()
-        for lo, hi in piece:
-            half = lo // half_cols
-            block = a_buf.at[half, :, lo - half * half_cols:hi - half * half_cols]
-            put_diag(part.at[0], dot(block[...], block[:TILE]), dot(block[TILE:], block[TILE:]), lo > 0)
+    for n, width, start in segments:
+        @pl.loop(0, n)
+        def _(c, width=width, start=start):
+            first_copy(width, start, c).wait()
+            half, cols, _ = first_load(start[0], width, c)
+            block = a_buf.at[half, :, cols]
+            put_diag(part.at[0], dot(block[...], block[:TILE]), dot(block[TILE:], block[TILE:]), True)
+
     pl.semaphore_wait(barrier, 3)
     send_partial(0)
 
@@ -290,7 +310,7 @@
 
     def local_gram(a_local):
         n_rows, local_cols = a_local.shape
-        assert n_rows == groups * BLK and local_cols == FIRST_LOADS[-1][1]
+        assert n_rows == groups * BLK and local_cols == sum(n * width for n, width in FIRST)
         sums = pl.pallas_call(
             gram_kernel,
             name="gram",
@@ -300,7 +320,7 @@
             scratch_shapes=[
                 pltpu.VMEM((6, BLK, local_cols // 2), jnp.bfloat16),
                 pltpu.VMEM((N_REMOTE, BLK, TILE), jnp.float32),
-                pltpu.SemaphoreType.DMA((len(FIRST_LOADS) + 2 * len(LOADS),)),
+                pltpu.SemaphoreType.DMA((N_FIRST + 2 * len(LOADS),)),
                 pltpu.SemaphoreType.DMA((N_STEPS,)),
                 pltpu.SemaphoreType.DMA((N_STEPS,)),
                 pltpu.SemaphoreType.DMA((N_REMOTE,)),

time: 87.7 us -> 86.1 us (0.982)
  Pallas kernels: 87.5 us -> 85.8 us
    pallas_call x1, Pallas kernels: 85.7 us -> 84 us  [local_gram(): pl.pallas_call(gram_kernel, name='gram', out_shape=[pltpu.VMEM((n, 2, BLK...]
where the time goes in v5:
time: 86.1 us; the launch traced here: 86 us
  Pallas kernels  85.8 us (100%)
    pallas_call x1, Pallas kernels, local_gram(): pl.pallas_call(gram_kernel, name='gram', out_shape=[pltpu.VMEM((n, 2, BLK...  84 us
    pallas_call x1, Pallas kernels, local_gram(): pl.pallas_call(place_kernel, name='place', out_shape=jax.ShapeDtypeStruct...  1.82 us

profile of v5, /device:TPU:1, one launch (start us, length us, event | category | flops | bytes accessed | tf_op | source)
XLA Modules:
  0.0 86.0 jit_solution(17406574013305139621)
XLA Ops:
  0.0 84.0 %gram.1 = (f32[3,2,512,256]{3,2,1,0:T(8,128)S(1)}, f32[2,2,512,256]{3,2,1,0:T(8,128)S(1)}, f32[3,2,512,256]{3,2,1,0:T(8,128)S(1)}) custom-call(bf16[2048,16384]{1,0:T(8,128)(2,1)} %a_ref.1), custom_call_target="tpu_custom_call" | custom-call | tf_op jit(solution)/shard_map/gram/pallas_call | solution.py:314
  84.0 1.8 %place.1 = f32[1,3,512,512]{3,2,1,0:T(8,128)} custom-call(f32[3,2,512,256]{3,2,1,0:T(8,128)S(1)} %get-tuple-element.8.own, f32[2,2,512,256]{3,2,1,0:T(8,128)S(1)} %get-tuple-element.9.part, f32[3,2,512,256]{3,2,1,0:T(8,128)S(1)} %get-tuple-element.10.recv), custom_call_target="tpu_custom_call" | custom-call | tf_op jit(solution)/shard_map/place/pallas_call | solution.py:333
